TPU v7x, 32 devices: a whole 2x2x4 slice. The times are simulated.
32 devices in a mesh: pod: 2 (over x), dp: 4 (over z), tp: 4 (over y, core).
Axes of the slice: x: 2, y: 2, z: 4, core: 2. Of those that a mesh axis runs over, the one named last changes fastest.
Arguments:
- x_saved: bfloat16 [12288, 1024], P(('pod', 'dp')), parts along dimension 0
- h_saved: bfloat16 [12288, 1024], P(('pod', 'dp')), parts along dimension 0
- mean_one: float32 [12288], P(('pod', 'dp')), parts along dimension 0
- rstd_one: float32 [12288], P(('pod', 'dp')), parts along dimension 0
- mean_two: float32 [12288], P(('pod', 'dp')), parts along dimension 0
- rstd_two: float32 [12288], P(('pod', 'dp')), parts along dimension 0
- gain_one: bfloat16 [1024], replicated
- gain_two: bfloat16 [1024], replicated
- grad_y: bfloat16 [12288, 1024], P(('pod', 'dp')), parts along dimension 0
- w_qkv: bfloat16 [1024, 3, 16, 64], P(None, None, 'tp')
- w_proj: bfloat16 [16, 64, 1024], P('tp')
- w_up: bfloat16 [1024, 4096], P(None, 'tp')
- w_down: bfloat16 [4096, 1024], P('tp')
Outputs:
- output 1: bfloat16 [12288, 1024], P(('pod', 'dp')), parts along dimension 0
- output 2: bfloat16 [2048, 3, 16, 64], P('pod', None, 'tp'), parts along dimension 0
- output 3: bfloat16 [32, 64, 1024], P(('pod', 'tp')), parts along dimension 0
- output 4: bfloat16 [2048, 4096], P('pod', 'tp'), parts along dimension 0
- output 5: bfloat16 [8192, 1024], P(('pod', 'tp')), parts along dimension 0
There are 2 independent parts. A program takes and returns all parts, laid end to end along the dimension named above; an argument that names none is the same for every part.
All inputs are finite; a program needn't handle non-finite values.
Results may differ from a plain program's by a relative error of at most 0.0170911.
Values are sent between devices in bfloat16 or wider.
A program may use at most 1 GiB of HBM per device.

v0:
```python
import math
import jax
import jax.numpy as jnp
from jax import lax
from jax.sharding import PartitionSpec as P

GELU_C = math.sqrt(2.0 / math.pi)


def layer_norm(row_vals, row_mean, row_rstd, gain_vec):
    x_hat = (row_vals.astype(jnp.float32) - row_mean[:, None]) * row_rstd[:, None]
    return x_hat, (x_hat * gain_vec.astype(jnp.float32)).astype(jnp.bfloat16)


def norm_back(d_norm, x_hat, row_rstd, gain_vec):
    scaled = d_norm * gain_vec.astype(jnp.float32)
    scaled_mean = jnp.mean(scaled, axis=-1, keepdims=True)
    proj_mean = jnp.mean(scaled * x_hat, axis=-1, keepdims=True)
    return row_rstd[:, None] * (scaled - scaled_mean - x_hat * proj_mean)


def gelu_pair(pre_act):
    pre_wide = pre_act.astype(jnp.float32)
    tanh_val = jnp.tanh(GELU_C * (pre_wide + 0.044715 * pre_wide * pre_wide * pre_wide))
    gelu_val = 0.5 * pre_wide * (1.0 + tanh_val)
    gelu_slope = 0.5 * (1.0 + tanh_val) + 0.5 * pre_wide * (1.0 - tanh_val * tanh_val) * GELU_C * (1.0 + 0.134145 * pre_wide * pre_wide)
    return gelu_val, gelu_slope


def causal_probs(q_heads, k_heads):
    tok_count = q_heads.shape[0]
    scores = jnp.einsum('qhe,khe->hqk', q_heads, k_heads, preferred_element_type=jnp.float32) * (q_heads.shape[-1] ** -0.5)
    row_ids = lax.broadcasted_iota(jnp.int32, (tok_count, tok_count), 0)
    col_ids = lax.broadcasted_iota(jnp.int32, (tok_count, tok_count), 1)
    scores = jnp.where(col_ids <= row_ids, scores, -1e30)
    shifted = jnp.exp(scores - jnp.max(scores, axis=-1, keepdims=True))
    return shifted / jnp.sum(shifted, axis=-1, keepdims=True)


def attn_grads(qkv_heads, prob_mat, prob_lo, d_attn):
    soft_scale = qkv_heads.shape[-1] ** -0.5
    dv_heads = jnp.einsum('hqk,qhe->khe', prob_lo, d_attn, preferred_element_type=jnp.float32).astype(jnp.bfloat16)
    d_probs = jnp.einsum('qhe,khe->hqk', d_attn, qkv_heads[:, 2], preferred_element_type=jnp.float32)
    d_scores = (prob_mat * (d_probs - jnp.sum(prob_mat * d_probs, axis=-1, keepdims=True)) * soft_scale).astype(jnp.bfloat16)
    dq_heads = jnp.einsum('hqk,khe->qhe', d_scores, qkv_heads[:, 1], preferred_element_type=jnp.float32).astype(jnp.bfloat16)
    dk_heads = jnp.einsum('hqk,qhe->khe', d_scores, qkv_heads[:, 0], preferred_element_type=jnp.float32).astype(jnp.bfloat16)
    return jnp.stack([dq_heads, dk_heads, dv_heads], axis=1)


def solution(mesh):
    row_spec = P(('pod', 'dp'), None)
    stat_spec = P(('pod', 'dp'))
    in_specs = (row_spec, row_spec, stat_spec, stat_spec, stat_spec, stat_spec, P(None), P(None), row_spec,
                P(None, None, 'tp', None), P('tp', None, None), P(None, 'tp'), P('tp', None))
    out_specs = (row_spec, P('pod', None, 'tp', None), P(('pod', 'tp'), None, None), P('pod', 'tp'), P(('pod', 'tp'), None))

    def local_step(x_saved, h_saved, mean_one, rstd_one, mean_two, rstd_two, gain_one, gain_two, grad_y, w_qkv, w_proj, w_up, w_down):
        hat_two, norm_two = layer_norm(h_saved, mean_two, rstd_two, gain_two)
        pre_act = jnp.dot(norm_two, w_up, preferred_element_type=jnp.float32).astype(jnp.bfloat16)
        gelu_val, gelu_slope = gelu_pair(pre_act)
        act_out = gelu_val.astype(jnp.bfloat16)
        d_act = lax.dot_general(grad_y, w_down, (((1,), (1,)), ((), ())), preferred_element_type=jnp.float32)
        d_pre = (d_act * gelu_slope).astype(jnp.bfloat16)
        grad_down = lax.dot_general(act_out, grad_y, (((0,), (0,)), ((), ())), preferred_element_type=jnp.float32)
        grad_up = lax.dot_general(norm_two, d_pre, (((0,), (0,)), ((), ())), preferred_element_type=jnp.float32)
        part_two = lax.dot_general(d_pre, w_up, (((1,), (1,)), ((), ())), preferred_element_type=jnp.float32).astype(jnp.bfloat16)
        d_norm_two = lax.psum(part_two, 'tp').astype(jnp.float32)
        d_mid = grad_y.astype(jnp.float32) + norm_back(d_norm_two, hat_two, rstd_two, gain_two)
        d_mid_lo = d_mid.astype(jnp.bfloat16)
        hat_one, norm_one = layer_norm(x_saved, mean_one, rstd_one, gain_one)
        qkv_heads = jnp.einsum('td,dche->tche', norm_one, w_qkv, preferred_element_type=jnp.float32).astype(jnp.bfloat16)
        prob_mat = causal_probs(qkv_heads[:, 0], qkv_heads[:, 1])
        prob_lo = prob_mat.astype(jnp.bfloat16)
        attn_out = jnp.einsum('hqk,khe->qhe', prob_lo, qkv_heads[:, 2], preferred_element_type=jnp.float32).astype(jnp.bfloat16)
        grad_proj = jnp.einsum('the,td->hed', attn_out, d_mid_lo, preferred_element_type=jnp.float32)
        d_attn = jnp.einsum('td,hed->the', d_mid_lo, w_proj, preferred_element_type=jnp.float32).astype(jnp.bfloat16)
        d_qkv = attn_grads(qkv_heads, prob_mat, prob_lo, d_attn)
        grad_qkv = jnp.einsum('td,tche->dche', norm_one, d_qkv, preferred_element_type=jnp.float32)
        part_one = jnp.einsum('tche,dche->td', d_qkv, w_qkv, preferred_element_type=jnp.float32).astype(jnp.bfloat16)
        d_norm_one = lax.psum(part_one, 'tp').astype(jnp.float32)
        grad_x = (d_mid + norm_back(d_norm_one, hat_one, rstd_one, gain_one)).astype(jnp.bfloat16)
        return (grad_x,
                lax.psum(grad_qkv, 'dp').astype(jnp.bfloat16),
                lax.psum(grad_proj, 'dp').astype(jnp.bfloat16),
                lax.psum(grad_up, 'dp').astype(jnp.bfloat16),
                lax.psum(grad_down, 'dp').astype(jnp.bfloat16))

    return jax.shard_map(local_step, mesh=mesh, in_specs=in_specs, out_specs=out_specs, check_vma=False)
```

profile of v0, /device:TPU:0, one launch (start us, length us, event | category | flops | bytes accessed | tf_op | source)
XLA Modules:
  0.0 715.4 jit_solution(7087693684839249016)
XLA Ops:
  8.8 5.6 convolution_convert_fusion.1
  14.4 6.9 fusion.27
  21.4 1.7 copy-done.22
  23.1 4.9 convolution_convert_fusion
  28.0 2.1 iota_compare_fusion
  30.2 8.7 %fusion.87 = f32[1024,1024]{1,0:T(8,128)} fusion(bf16[1536,1024]{1,0:T(8,128)(2,1)} %copy-done.22, bf16[1536,1024]{1,0:T(8,128)(2,1)} %param.14, f32[1024]{0:T(1024)S(1)} %convert_element_type.103, f32[1536]{0:T(1024)S(1)} %copy-done.13, f32[1536]{0:T(1024)S(1)} %copy-done.14), kind=kOutput, calls=%fused_computation.93 | convolution fusion | flops 3229089792 | bytes 10502144 | tf_op jit(solution)/shard_map/dot_general | solution.py:65
  38.9 5.8 fusion.34
  44.7 2.9 fusion.89
  47.7 1.7 convert_element_type.113
  49.3 21.9 %exponential_reduce_fusion = (f32[4,1536]{1,0:T(4,128)S(1)}, f32[4,1536,1536]{1,2,0:T(8,128)}) fusion(pred[1536,1536]{0,1:T(8,128)(4,1)} %iota_compare_fusion, bf16[1536,3,4,64]{0,3,2,1:T(8,128)(2,1)} %convert_element_type.113), kind=kOutput, calls=%fused_computation.11 | convolution fusion | flops 1245709824 | bytes 41705472 | tf_op jit(solution)/shard_map/sub | solution.py:36
  71.2 27.9 %all-reduce.5.cloned.1.call-done = bf16[1536,1024]{1,0:T(8,128)(2,1)} async-done(((bf16[1536,1024]{1,0:T(8,128)(2,1)}), bf16[1536,1024]{1,0:T(8,128)(2,1)}) %all-reduce.5.cloned.1.call-update) | async-done | bytes 3145744 | tf_op jit(solution)/shard_map/psum | solution.py:67
  99.2 4.9 fusion.33
  104.1 4.5 multiply_add_fusion
  108.6 2.7 copy-done.2
  112.4 16.0 %fusion.75 = f32[4,1536,1536]{1,2,0:T(8,128)} fusion(bf16[1536,4,64]{0,2,1:T(8,128)(2,1)S(1)} %fusion.56, bf16[1536,3,4,64]{0,3,2,1:T(8,128)(2,1)} %convert_element_type.113), kind=kOutput, calls=%fused_computation.77 | convolution fusion | flops 1207959552 | bytes 39321600 | tf_op jit(solution)/shard_map/qhe,khe->hqk/dot_general | solution.py:43
  128.4 19.5 %fusion.64 = bf16[1536,1,4,64]{0,3,2,1:T(8,128)(2,1)S(1)} fusion(bf16[1536,4,64]{0,2,1:T(8,128)(2,1)S(1)} %fusion.56, f32[4,1536]{1,0:T(4,128)S(1)} %get-tuple-element.13, pred[1536,1536]{0,1:T(8,128)(4,1)} %iota_compare_fusion, bf16[1536,3,4,64]{0,3,2,1:T(8,128)(2,1)} %convert_element_type.113), kind=kOutput, calls=%fused_computation.68 | convolution fusion | flops 2463505920 | bytes 5529600 | tf_op jit(solution)/shard_map/hqk,qhe->khe/dot_general | solution.py:42
  147.8 48.5 %fusion.67 = bf16[1536,1,4,64]{0,3,2,1:T(8,128)(2,1)S(1)} fusion(f32[4,1536,1536]{1,2,0:T(8,128)} %fusion.75, bf16[1536,3,4,64]{0,3,2,1:T(8,128)(2,1)} %convert_element_type.113, f32[4,1536,1536]{1,2,0:T(8,128)} %get-tuple-element.14, f32[4,1536]{1,0:T(4,128)S(1)} %get-tuple-element.13), kind=kOutput, calls=%fused_computation.69 | convolution fusion | flops 1274420736 | bytes 152616960 | tf_op jit(solution)/shard_map/hqk,qhe->khe/dot_general | solution.py:46
  196.3 48.1 %fusion.70 = bf16[1536,1,4,64]{0,3,2,1:T(8,128)(2,1)S(1)} fusion(f32[4,1536,1536]{1,2,0:T(8,128)} %fusion.75, bf16[1536,3,4,64]{0,3,2,1:T(8,128)(2,1)} %convert_element_type.113, f32[4,1536,1536]{1,2,0:T(8,128)} %get-tuple-element.14, f32[4,1536]{1,0:T(4,128)S(1)} %get-tuple-element.13), kind=kOutput, calls=%fused_computation.70 | convolution fusion | flops 1274420736 | bytes 152616960 | tf_op jit(solution)/shard_map/hqk,khe->qhe/dot_general | solution.py:45
  244.5 5.4 bitcast_convert_fusion
  251.6 17.3 %fusion.36 = f32[4,64,1024]{2,1,0:T(8,128)S(1)} fusion(f32[1536,1024]{1,0:T(8,128)} %copy-done.2, bf16[1536,3,4,64]{0,3,2,1:T(8,128)(2,1)} %convert_element_type.113, f32[4,1536,1536]{1,2,0:T(8,128)} %get-tuple-element.14, f32[4,1536]{1,0:T(4,128)S(1)} %get-tuple-element.13), kind=kOutput, calls=%fused_computation.54 | convolution fusion | flops 2034106368 | bytes 45899776 | tf_op jit(solution)/shard_map/the,td->hed/dot_general | solution.py:75
  269.0 7.0 fusion.88
  276.0 421.4 %all-reduce.8 = (bf16[1024,3,4,64]{0,3,2,1:T(8,128)(2,1)}, bf16[4,64,1024]{2,1,0:T(8,128)(2,1)}, bf16[1024,1024]{1,0:T(8,128)(2,1)}, bf16[1024,1024]{1,0:T(8,128)(2,1)}) all-reduce(f32[1024,3,4,64]{0,3,2,1:T(8,128)} %bitcast.76, f32[4,64,1024]{2,1,0:T(8,128)S(1)} %fusion.36, ...), channel_id=1, replica_groups=mesh['pod'=2,'dp'=4,'tp'=4] {'dp'}, use_global_device_ids=true, to_apply=%region_9.10 | all-reduce | flops 3145728 | bytes 18874368 | tf_op jit(solution)/shard_map/psum | solution.py:83
  697.4 5.1 fusion.32
  702.5 5.6 add_convert_fusion
  (60 shorter events, 4.5 us)
Async XLA Ops:
  7.2 92.0 %all-reduce.5.cloned.1.call-start = ((), (), s32[]{:S(2)}) async-start(), calls=%async_computation | async-start | bytes 6291456 | tf_op jit(solution)/shard_map/psum | solution.py:67
  8.8 5.6 copy-start.8
  8.8 5.6 copy-start.20
  14.4 6.9 copy-start.23
  23.1 7.1 copy-start.13
  23.1 7.1 copy-start.14
  28.0 669.4 %all-reduce.7.cloned.1.call-start = ((), (), s32[]{:S(2)}) async-start(), calls=%async_computation.1 | async-start | bytes 6291456 | tf_op jit(solution)/shard_map/psum | solution.py:80
  30.1 8.7 %copy-start.9 = (bf16[1536,1024]{1,0:T(8,128)(2,1)S(1)}, bf16[1536,1024]{1,0:T(8,128)(2,1)}, u32[]{:S(2)}) copy-start(bf16[1536,1024]{1,0:T(8,128)(2,1)} %param.21) | copy-start | bytes 9437188
  30.1 8.7 %copy-start.24 = (bf16[1536,1024]{1,0:T(8,128)(2,1)S(1)}, bf16[1536,1024]{1,0:T(8,128)(2,1)}, u32[]{:S(2)}) copy-start(bf16[1536,1024]{1,0:T(8,128)(2,1)} %copy-done.23) | copy-start | bytes 9437188
  38.9 5.8 copy-start.19
  38.9 5.8 copy-start.4
  38.9 5.8 copy-start.15
  38.9 5.8 copy-start.17
  38.9 5.8 copy-start.21
  44.7 2.9 copy-start.11
  99.2 4.9 copy-start.3
  99.2 4.9 copy-start.6
  104.1 7.3 %copy-start.10 = (bf16[4,64,1024]{2,1,0:T(8,128)(2,1)S(1)}, bf16[4,64,1024]{2,1,0:T(8,128)(2,1)}, u32[]{:S(2)}) copy-start(bf16[4,64,1024]{2,1,0:T(8,128)(2,1)} %param.23) | copy-start | bytes 1572868
  251.6 17.3 %copy-start.12 = (f32[1024]{0:T(1024)S(1)}, f32[1024]{0:T(1024)}, u32[]{:S(2)}) copy-start(f32[1024]{0:T(1024)} %copy-done.11) | copy-start | bytes 12292
  251.6 17.3 %copy-start.16 = (f32[1536]{0:T(1024)S(1)}, f32[1536]{0:T(1024)}, u32[]{:S(2)}) copy-start(f32[1536]{0:T(1024)} %param.15) | copy-start | bytes 18436
  251.6 17.4 %copy-start.18 = (f32[1536]{0:T(1024)S(1)}, f32[1536]{0:T(1024)}, u32[]{:S(2)}) copy-start(f32[1536]{0:T(1024)} %param.16) | copy-start | bytes 18436
  697.4 5.1 copy-start.5
  697.4 5.1 copy-start.7
  702.5 5.7 copy-start.1
  (3 other events, 6.1 us)
Sparse Core Ops, SparseCore 0:
  28.1 71.0 all-reduce.4
  269.0 68.3 all-reduce.6
where the time goes:
time: 724 us; the launch traced here: 715 us
  blocking collectives  421 us (58%)
  matrix products  220 us (30%)
  waiting for transfers between devices  28 us (4%)
  other arithmetic  26.4 us (4%)
  between operations  14.8 us (2%)
    psum x1, blocking collectives, local_step(): lax.psum(grad_qkv, 'dp').astype(jnp.bfloat16)  421 us
    dot_general x1, matrix products, attn_grads(): jnp.einsum('hqk,qhe->khe', d_scores, qkv_heads[:, 0], preferred_element_t...  48.5 us
    dot_general x1, matrix products, attn_grads(): jnp.einsum('hqk,khe->qhe', d_scores, qkv_heads[:, 1], preferred_element_t...  48.1 us
    psum x1, waiting for transfers between devices, local_step(): d_norm_two = lax.psum(part_two, 'tp').astype(jnp.float32)  27.9 us
    sub x1, matrix products, causal_probs(): shifted = jnp.exp(scores - jnp.max(scores, axis=-1, keepdims=True))  21.9 us
    dot_general x1, matrix products, attn_grads(): jnp.einsum('hqk,qhe->khe', prob_lo, d_attn, preferred_element_type=jnp.fl...  19.5 us
    dot_general x1, matrix products, local_step(): jnp.einsum('the,td->hed', attn_out, d_mid_lo, preferred_element_type=jnp....  17.3 us
    dot_general x1, matrix products, attn_grads(): jnp.einsum('qhe,khe->hqk', d_attn, qkv_heads[:, 2], preferred_element_typ...  16 us
  transfers between devices with their start and end apart: 2, of which 1 were waited for; matrix products, arithmetic and copies ran while one was open for 7% of the time, Pallas kernels for 0%

commit v1 on v0

v1 whole, which is shorter than its diff:
```python
import functools
import math
import jax
import jax.numpy as jnp
from jax import lax
from jax.experimental import pallas as pl
from jax.experimental.pallas import tpu as pltpu
from jax.sharding import PartitionSpec as P

GELU_C = math.sqrt(2.0 / math.pi)
MESH = pl.DeviceIdType.MESH
F32 = jnp.float32
BF16 = jnp.bfloat16

TOK = 1536
DIM = 1024
BLK = 256
HALF = TOK // 2
NBLK = TOK // BLK
HBLK = HALF // BLK
CROWS = 32
ROWS = 3072
CHUNKS = ROWS // (2 * CROWS)
SLOTS = 16
STAGES = 8
LAG = 2
DP = 4
STEPS = CHUNKS + 2 * LAG * (DP - 1)


def dot_nn(a, b):
    return lax.dot_general(a, b, (((1,), (0,)), ((), ())), preferred_element_type=F32)


def dot_nt(a, b):
    return lax.dot_general(a, b, (((1,), (1,)), ((), ())), preferred_element_type=F32)


def dot_tn(a, b):
    return lax.dot_general(a, b, (((0,), (0,)), ((), ())), preferred_element_type=F32)


def layer_kernel(x_ref, h_ref, dy_ref, st_ref, gn_ref, wq_ref, wo_ref, w1_ref, w2_ref,
                 dx_ref, fb_ref,
                 gb, land, stage, nrm, part, recv_a, recv_b, recv_c, dh_f, dh_b,
                 ch_send, ch_recv, ch_free, fb_send, fb_recv, st_copy,
                 pa_send, pa_recv, pb_send, pb_recv, pd_send, pd_recv, dx_copy):
    pod, z, tp = lax.axis_index('pod'), lax.axis_index('dp'), lax.axis_index('tp')
    core = lax.rem(tp, 2)
    mate = (pod, z, tp + 1 - 2 * core)
    peer = (pod, z, lax.rem(tp + 2, 4))
    z_hi = jnp.minimum(z + 1, DP - 1)
    z_lo = jnp.maximum(z - 1, 0)
    own0 = core * HALF
    par0 = HALF - own0

    barrier = pltpu.get_barrier_semaphore()
    for dev in (mate, peer):
        pl.semaphore_signal(barrier, inc=1, device_id=dev, device_id_type=MESH)
    pl.when(z < DP - 1)(lambda: pl.semaphore_signal(barrier, inc=1, device_id=(pod, z_hi, tp), device_id_type=MESH))
    pl.when(z > 0)(lambda: pl.semaphore_signal(barrier, inc=1, device_id=(pod, z_lo, tp), device_id_type=MESH))
    pl.semaphore_wait(barrier, 2 + jnp.where(z < DP - 1, 1, 0) + jnp.where(z > 0, 1, 0))

    def way_of(way):
        if way == 0:
            return z, (pod, z_hi, tp), (pod, z_lo, tp)
        return DP - 1 - z, (pod, z_lo, tp), (pod, z_hi, tp)

    def rows_of(way, c):
        return pl.ds(pl.multiple_of(c * (2 * CROWS) + way * CROWS, CROWS), CROWS)

    def chain_copy(way, c, nxt):
        slot = lax.rem(c, SLOTS)
        return pltpu.make_async_remote_copy(
            src_ref=gb.at[rows_of(way, c)], dst_ref=land.at[way, slot], send_sem=ch_send.at[way, slot],
            recv_sem=ch_recv.at[way, slot], device_id=nxt, device_id_type=MESH)

    def total_copy(way, c, prv):
        return pltpu.make_async_remote_copy(
            src_ref=stage.at[way, lax.rem(c, STAGES)], dst_ref=fb_ref.at[rows_of(way, c)], send_sem=fb_send.at[way, c],
            recv_sem=fb_recv.at[way, c], device_id=prv, device_id_type=MESH)

    def pass_copy(way, c, prv):
        return pltpu.make_async_remote_copy(
            src_ref=fb_ref.at[rows_of(way, c)], dst_ref=fb_ref.at[rows_of(way, c)], send_sem=fb_send.at[way, c],
            recv_sem=fb_recv.at[way, c], device_id=prv, device_id_type=MESH)

    def keep_copy(way, c):
        slot = lax.rem(c, STAGES)
        return pltpu.make_async_copy(stage.at[way, slot], fb_ref.at[rows_of(way, c)], st_copy.at[way, slot])

    def chain_step(s):
        for way in (0, 1):
            pos, nxt, prv = way_of(way)
            c = s - LAG * pos

            @pl.when((c >= 0) & (c < CHUNKS))
            def _():
                @pl.when(pos > 0)
                def _():
                    chain_copy(way, c, nxt).wait_recv()
                    gb[rows_of(way, c), :] += land[way, lax.rem(c, SLOTS)]

                    @pl.when(c < CHUNKS - SLOTS)
                    def _():
                        pl.semaphore_signal(ch_free.at[way], inc=1, device_id=prv, device_id_type=MESH)

                @pl.when(pos < DP - 1)
                def _():
                    @pl.when(c >= SLOTS)
                    def _():
                        pl.semaphore_wait(ch_free.at[way], 1)
                        chain_copy(way, c - SLOTS, nxt).wait_send()
                    chain_copy(way, c, nxt).start()

                @pl.when(pos == DP - 1)
                def _():
                    @pl.when(c >= STAGES)
                    def _():
                        total_copy(way, c - STAGES, prv).wait_send()
                        keep_copy(way, c - STAGES).wait()
                    stage[way, lax.rem(c, STAGES)] = gb[rows_of(way, c), :].astype(BF16)
                    total_copy(way, c, prv).start()
                    keep_copy(way, c).start()

            c2 = s - LAG * (2 * (DP - 1) - pos)

            @pl.when((pos < DP - 1) & (c2 >= 0) & (c2 < CHUNKS))
            def _():
                pass_copy(way, c2, prv).wait_recv()

                @pl.when(pos > 0)
                def _():
                    pass_copy(way, c2, prv).start()

    def chain_steps(s0, n):
        def body(k, carry):
            chain_step(s0 + k)
            return carry
        lax.fori_loop(0, n, body, 0)

    def chain_end():
        for way in (0, 1):
            pos, nxt, prv = way_of(way)

            @pl.when(pos < DP - 1)
            def _():
                def body(c, carry):
                    chain_copy(way, c, nxt).wait_send()
                    return carry
                lax.fori_loop(CHUNKS - SLOTS, CHUNKS, body, 0)

            @pl.when(pos == DP - 1)
            def _():
                def body(c, carry):
                    total_copy(way, c, prv).wait_send()
                    keep_copy(way, c).wait()
                    return carry
                lax.fori_loop(CHUNKS - STAGES, CHUNKS, body, 0)

            @pl.when((pos > 0) & (pos < DP - 1))
            def _():
                def body(c, carry):
                    pass_copy(way, c, prv).wait_send()
                    return carry
                lax.fori_loop(0, CHUNKS, body, 0)

    def rows(i):
        return pl.ds(pl.multiple_of(i * BLK, BLK), BLK)

    def at(base, b):
        return pl.ds(pl.multiple_of(base + b * BLK, BLK), BLK)

    def hat(ref, rs, k):
        return (ref[rs, :].astype(F32) - st_ref[rs, k:k + 1]) * st_ref[rs, k + 1:k + 2]

    def norm_back(d_norm, x_hat, rstd, gain):
        scaled = d_norm * gain
        scaled_mean = jnp.mean(scaled, axis=-1, keepdims=True)
        proj_mean = jnp.mean(scaled * x_hat, axis=-1, keepdims=True)
        return rstd * (scaled - scaled_mean - x_hat * proj_mean)

    def gain(k):
        return gn_ref[k:k + 1, :].astype(F32)

    def mate_copy(rnd, b):
        return pltpu.make_async_remote_copy(
            src_ref=part.at[at(par0, b)], dst_ref=recv_a.at[b], send_sem=pa_send.at[rnd, b],
            recv_sem=pa_recv.at[rnd, b], device_id=mate, device_id_type=MESH)

    def peer_copy(rnd, b):
        dst = (recv_b, recv_c)[rnd]
        return pltpu.make_async_remote_copy(
            src_ref=part.at[at(own0, b)], dst_ref=dst.at[b], send_sem=pb_send.at[rnd, b],
            recv_sem=pb_recv.at[rnd, b], device_id=peer, device_id_type=MESH)

    def chip_sum(rnd, b):
        mate_copy(rnd, b).wait_recv()
        ro = at(own0, b)
        part[ro, :] = (part[ro, :].astype(F32) + recv_a[b].astype(F32)).astype(BF16)
        peer_copy(rnd, b).start()

    def part_block(rnd, b, fn):
        rp = at(par0, b)
        part[rp, :] = fn(rp).astype(BF16)
        mate_copy(rnd, b).start()
        ro = at(own0, b)
        part[ro, :] = fn(ro).astype(BF16)

    def mlp(act_s, da_s):
        def fwd(i, carry):
            rs = rows(i)
            n2 = (hat(h_ref, rs, 2) * gain(1)).astype(BF16)
            nrm[rs, :] = n2
            pre = dot_nn(n2, w1_ref[...]).astype(BF16).astype(F32)
            th = jnp.tanh(GELU_C * (pre + 0.044715 * pre * pre * pre))
            act_s[rs, :] = (0.5 * pre * (1.0 + th)).astype(BF16)
            slope = 0.5 * (1.0 + th) + 0.5 * pre * (1.0 - th * th) * GELU_C * (1.0 + 0.134145 * pre * pre)
            da_s[rs, :] = (dot_nt(dy_ref[rs, :], w2_ref[...]) * slope).astype(BF16)
            return carry
        lax.fori_loop(0, NBLK, fwd, 0)

        def down(j, carry):
            gb[rows(j), :] = dot_tn(act_s[:, rows(j)], dy_ref[...])
            pl.when(lax.rem(j, 2) == 1)(lambda: chain_step(lax.div(j, 2)))
            return carry
        lax.fori_loop(0, DIM // BLK, down, 0)

        def dn2(b, carry):
            part_block(0, b, lambda rs: dot_nt(da_s[rs, :], w1_ref[...]))
            pl.when(b > 0)(lambda: chip_sum(0, b - 1))
            chain_step(2 + b)
            return carry
        lax.fori_loop(0, HBLK, dn2, 0)
        chip_sum(0, HBLK - 1)

        def up(j, carry):
            gb[at(DIM, j), :] = dot_tn(nrm[:, rows(j)], da_s[...])
            pl.when(lax.rem(j, 2) == 1)(lambda: chain_step(5 + lax.div(j, 2)))
            return carry
        lax.fori_loop(0, DIM // BLK, up, 0)

    pl.run_scoped(mlp, pltpu.VMEM((TOK, DIM), BF16), pltpu.VMEM((TOK, DIM), BF16))

    def mid_copy(b):
        return pltpu.make_async_remote_copy(
            src_ref=dh_b.at[at(own0, b)], dst_ref=dh_b.at[at(own0, b)], send_sem=pd_send.at[0, b],
            recv_sem=pd_recv.at[0, b], device_id=mate, device_id_type=MESH)

    def out_copy(b):
        return pltpu.make_async_remote_copy(
            src_ref=part.at[at(own0, b)], dst_ref=dx_ref.at[at(own0, b)], send_sem=pd_send.at[1, b],
            recv_sem=pd_recv.at[1, b], device_id=mate, device_id_type=MESH)

    def out_keep(b):
        return pltpu.make_async_copy(part.at[at(own0, b)], dx_ref.at[at(own0, b)], dx_copy.at[b])

    def attention(qkv, d_qkv, o_s, do_s, acc_k, acc_v):
        def proj(i, carry):
            rs = rows(i)
            n1 = (hat(x_ref, rs, 0) * gain(0)).astype(BF16)
            nrm[rs, :] = n1
            qkv[rs, :] = dot_nt(n1, wq_ref[...]).astype(BF16)
            pl.when(lax.rem(i, 2) == 1)(lambda: chain_step(7 + lax.div(i, 2)))
            return carry
        lax.fori_loop(0, NBLK, proj, 0)

        def mid(b, carry):
            chain_step(10 + 2 * b)
            chain_step(11 + 2 * b)
            peer_copy(0, b).wait_recv()
            ro = at(own0, b)
            d_norm = part[ro, :].astype(F32) + recv_b[b].astype(F32)
            dh = dy_ref[ro, :].astype(F32) + norm_back(d_norm, hat(h_ref, ro, 2), st_ref[ro, 3:4], gain(1))
            dh_f[rows(b), :] = dh
            dh_b[ro, :] = dh.astype(BF16)
            mid_copy(b).start()
            return carry
        lax.fori_loop(0, HBLK, mid, 0)
        for b in range(HBLK):
            mid_copy(b).wait_recv()

        def d_out(i, carry):
            do_s[rows(i), :] = dot_nt(dh_b[rows(i), :], wo_ref[...]).astype(BF16)
            return carry
        lax.fori_loop(0, NBLK, d_out, 0)

        lane = lax.broadcasted_iota(jnp.int32, (BLK, 128), 1)
        causal = lax.broadcasted_iota(jnp.int32, (BLK, BLK), 1) <= lax.broadcasted_iota(jnp.int32, (BLK, BLK), 0)
        zero = jnp.zeros((BLK, 128), BF16)

        def pair(p, carry):
            def cols(k):
                return pl.ds(pl.multiple_of(k * 256 + p * 128, 128), 128)
            for n, i in enumerate(reversed(range(NBLK))):
                span = (i + 1) * BLK
                rs = slice(i * BLK, span)
                k_all = qkv[0:span, cols(1)]
                v_all = qkv[0:span, cols(2)]
                outs, dqs = [], []
                dk = dv = None
                for hh in (0, 1):
                    mine = (lane < 64) if hh == 0 else (lane >= 64)
                    q = jnp.where(mine, qkv[rs, cols(0)], zero)
                    do = jnp.where(mine, do_s[rs, cols(0)], zero)
                    sc = dot_nt(q, k_all) * 0.125
                    last = jnp.where(causal, sc[:, span - BLK:], -1e30)
                    sc = jnp.concatenate([sc[:, :span - BLK], last], axis=1) if i else last
                    ex = jnp.exp(sc - jnp.max(sc, axis=-1, keepdims=True))
                    prob = ex * (1.0 / jnp.sum(ex, axis=-1, keepdims=True))
                    prob_lo = prob.astype(BF16)
                    outs.append(dot_nn(prob_lo, v_all))
                    dp = dot_nt(do, v_all)
                    ds = (prob * (dp - jnp.sum(prob * dp, axis=-1, keepdims=True)) * 0.125).astype(BF16)
                    dqs.append(dot_nn(ds, k_all))
                    dv_h = dot_tn(prob_lo, do)
                    dk_h = dot_tn(ds, q)
                    if i == NBLK - 1 and hh == 0:
                        acc_v[...] = dv_h
                        acc_k[...] = dk_h
                    else:
                        acc_v[0:span, :] += dv_h
                        acc_k[0:span, :] += dk_h
                o_s[rs, cols(0)] = jnp.where(lane < 64, outs[0], outs[1]).astype(BF16)
                d_qkv[rs, cols(0)] = jnp.where(lane < 64, dqs[0], dqs[1]).astype(BF16)
                chain_step(16 + p * NBLK + n)
            d_qkv[:, cols(1)] = acc_k[...].astype(BF16)
            d_qkv[:, cols(2)] = acc_v[...].astype(BF16)
            return carry
        lax.fori_loop(0, 2, pair, 0)

        gb[2 * DIM:2 * DIM + BLK, :] = dot_tn(o_s[...], dh_b[...])
        chain_step(28)

        def w_qkv(j, carry):
            gb[at(2 * DIM + BLK, j), :] = dot_tn(d_qkv[:, rows(j)], nrm[...])
            chain_step(29 + j)
            return carry
        lax.fori_loop(0, 3, w_qkv, 0)

        for b in range(HBLK):
            mate_copy(0, b).wait_send()
            peer_copy(0, b).wait_send()
            mid_copy(b).wait_send()

        def dn1(b, carry):
            part_block(1, b, lambda rs: dot_nn(d_qkv[rs, :], wq_ref[...]))
            pl.when(b > 0)(lambda: chip_sum(1, b - 1))
            chain_step(32 + b)
            return carry
        lax.fori_loop(0, HBLK, dn1, 0)
        chip_sum(1, HBLK - 1)

    pl.run_scoped(attention, pltpu.VMEM((TOK, 768), BF16), pltpu.VMEM((TOK, 768), BF16),
                  pltpu.VMEM((TOK, BLK), BF16), pltpu.VMEM((TOK, BLK), BF16),
                  pltpu.VMEM((TOK, 128), F32), pltpu.VMEM((TOK, 128), F32))

    def final(b, carry):
        chain_step(35 + 3 * b)
        chain_step(36 + 3 * b)
        chain_step(37 + 3 * b)
        peer_copy(1, b).wait_recv()
        peer_copy(1, b).wait_send()
        ro = at(own0, b)
        d_norm = part[ro, :].astype(F32) + recv_c[b].astype(F32)
        dx = dh_f[rows(b), :] + norm_back(d_norm, hat(x_ref, ro, 0), st_ref[ro, 1:2], gain(0))
        part[ro, :] = dx.astype(BF16)
        out_copy(b).start()
        out_keep(b).start()
        return carry
    lax.fori_loop(0, HBLK, final, 0)
    chain_steps(35 + 3 * HBLK, STEPS - 35 - 3 * HBLK)
    chain_end()
    for b in range(HBLK):
        mate_copy(1, b).wait_send()
        out_copy(b).wait()
        out_keep(b).wait()


def solution(mesh):
    row_spec = P(('pod', 'dp'), None)
    stat_spec = P(('pod', 'dp'))
    in_specs = (row_spec, row_spec, stat_spec, stat_spec, stat_spec, stat_spec, P(None), P(None), row_spec,
                P(None, None, 'tp', None), P('tp', None, None), P(None, 'tp'), P('tp', None))
    out_specs = (row_spec, P('pod', None, 'tp', None), P(('pod', 'tp'), None, None), P('pod', 'tp'), P(('pod', 'tp'), None))

    vmem = pl.BlockSpec(memory_space=pltpu.VMEM)
    hbm = pl.BlockSpec(memory_space=pl.ANY)
    dma = pltpu.SemaphoreType.DMA
    scratch = [
        pltpu.VMEM((ROWS, DIM), F32),
        pltpu.VMEM((2, SLOTS, CROWS, DIM), F32),
        pltpu.VMEM((2, STAGES, CROWS, DIM), BF16),
        pltpu.VMEM((TOK, DIM), BF16),
        pltpu.VMEM((TOK, DIM), BF16),
        pltpu.VMEM((HBLK, BLK, DIM), BF16),
        pltpu.VMEM((HBLK, BLK, DIM), BF16),
        pltpu.VMEM((HBLK, BLK, DIM), BF16),
        pltpu.VMEM((HALF, DIM), F32),
        pltpu.VMEM((TOK, DIM), BF16),
        dma((2, SLOTS)), dma((2, SLOTS)), pltpu.SemaphoreType.REGULAR((2,)),
        dma((2, CHUNKS)), dma((2, CHUNKS)), dma((2, STAGES)),
        dma((2, HBLK)), dma((2, HBLK)), dma((2, HBLK)), dma((2, HBLK)),
        dma((2, HBLK)), dma((2, HBLK)), dma((HBLK,)),
    ]
    layer = pl.pallas_call(
        layer_kernel,
        out_shape=(jax.ShapeDtypeStruct((TOK, DIM), BF16), jax.ShapeDtypeStruct((ROWS, DIM), BF16)),
        in_specs=[vmem] * 9,
        out_specs=(hbm, hbm),
        scratch_shapes=scratch,
        compiler_params=pltpu.CompilerParams(collective_id=0, has_side_effects=True, vmem_limit_bytes=67043328),
        name='layer_backward')

    def local_step(x_saved, h_saved, mean_one, rstd_one, mean_two, rstd_two, gain_one, gain_two, grad_y, w_qkv, w_proj, w_up, w_down):
        stats = jnp.stack([mean_one, rstd_one, mean_two, rstd_two], axis=1)
        gains = jnp.stack([gain_one, gain_two], axis=0)
        wq_t = jnp.transpose(w_qkv, (1, 2, 3, 0)).reshape(768, DIM)
        grad_x, grads = layer(x_saved, h_saved, grad_y, stats, gains, wq_t, w_proj.reshape(BLK, DIM), w_up, w_down)
        grad_qkv = jnp.transpose(grads[2 * DIM + BLK:].reshape(3, 4, 64, DIM), (3, 0, 1, 2))
        return (grad_x, grad_qkv, grads[2 * DIM:2 * DIM + BLK].reshape(4, 64, DIM), grads[DIM:2 * DIM], grads[:DIM])

    return jax.shard_map(local_step, mesh=mesh, in_specs=in_specs, out_specs=out_specs, check_vma=False)
```

time: 724 us -> 265 us (0.37); the launches traced: 715 us -> 265 us
  blocking collectives: 421 us -> 0 us
  Pallas kernels: 0 us -> 247 us
  matrix products: 220 us -> 0 us
  waiting for transfers between devices: 28 us -> 0 us
  other arithmetic: 26.4 us -> 0.64 us
  between operations: 14.8 us -> 0.65 us
  local copies, waits for them, and re-layouts: 5.27 us -> 16.4 us
    psum x1 -> x0, blocking collectives: 421 us -> none  [local_step(): lax.psum(grad_qkv, 'dp').astype(jnp.bfloat16)]
    pallas_call x0 -> x1, Pallas kernels: none -> 247 us  [local_step(): layer(x_saved, h_saved, grad_y, stats, gains, wq_t, w_proj.reshape(BLK, D...]
    dot_general x12 -> x0, matrix products: 188 us -> none  [the longest x1 48.5 us: attn_grads(): jnp.einsum('hqk,qhe->khe', d_scores, qkv_heads[:, 0], preferred_element_t...]
    psum x2 -> x0, waiting for transfers between devices: 27.9 us -> none  [the longest x1 27.9 us: local_step(): d_norm_two = lax.psum(part_two, 'tp').astype(jnp.float32)]
    sub x1 -> x0, matrix products: 21.9 us -> none  [causal_probs(): shifted = jnp.exp(scores - jnp.max(scores, axis=-1, keepdims=True))]
    reduce_sum x2 -> x0, other arithmetic: 9.94 us -> none  [norm_back(): scaled_mean = jnp.mean(scaled, axis=-1, keepdims=True)]
    unnamed x2 -> x0, matrix products: 9.93 us -> none
    slice x0 -> x3, local copies, waits for them, and re-layouts: none -> 9.37 us  [the longest x1 4.83 us: local_step(): grads[:DIM]]
  transfers between devices with their start and end apart: 2 -> 0, of which waited for: 1 -> 0; matrix products, arithmetic and copies ran while one was open for 7% -> 0% of each run, Pallas kernels for 0% -> 0%
where the time goes in v1:
time: 265 us
  Pallas kernels  247 us (93%)
  local copies, waits for them, and re-layouts  16.4 us (6%)
    pallas_call x1, Pallas kernels, local_step(): layer(x_saved, h_saved, grad_y, stats, gains, wq_t, w_proj.reshape(BLK, D...  247 us

profile of v1, /device:TPU:0, one launch (start us, length us, event | category | flops | bytes accessed | tf_op | source)
XLA Modules:
  0.0 264.8 jit_solution(11928392713074455100)
XLA Ops:
  0.6 0.7 stack.29
  1.3 0.7 stack.30
  2.0 0.6 pad_maximum_fusion.1.gn_ref
  2.6 0.7 stack.24
  3.3 0.7 stack.25
  4.0 0.7 stack.26
  4.7 0.7 stack.27
  5.4 1.2 copy.22.st_ref
  6.6 247.2 %layer_backward.1 = (bf16[1536,1024]{1,0:T(8,128)(2,1)}, bf16[3072,1024]{1,0:T(8,128)(2,1)}) custom-call(bf16[1536,1024]{1,0:T(8,128)(2,1)} %x_ref.1, bf16[1536,1024]{1,0:T(8,128)(2,1)} %h_ref.1, bf16[1536,1024]{1,0:T(8,128)(2,1)} %dy_ref.1, f32[1536,4]{1,0:T(8,128)} %copy.22.st_ref, bf16[2,1024]{1,0:T(2,128)(2,1)} %pad_maximum_fusion.1.gn_ref, ...), custom_call_target="tpu_custom_call" | custom-call | tf_op jit(solution)/shard_map/layer_backward/pallas_call | solution.py:419
  253.8 1.9 slice.13
  255.7 2.7 %slice.12 = bf16[768,1024]{1,0:T(8,128)(2,1)} slice(bf16[3072,1024]{1,0:T(8,128)(2,1)} %get-tuple-element.8), slice={[2304:3072], [0:1024]} | slice | bytes 3145728 | tf_op jit(solution)/shard_map/slice | solution.py:420
  258.3 0.0 copy-start
  258.3 4.8 %fusion = (bf16[1024,1024]{1,0:T(8,128)(2,1)}, bf16[1024,1024]{1,0:T(8,128)(2,1)}) fusion(bf16[3072,1024]{1,0:T(8,128)(2,1)} %get-tuple-element.8), kind=kLoop, calls=%fused_computation.2 | loop fusion | bytes 8388608 | tf_op jit(solution)/shard_map/slice | solution.py:421
  263.2 0.0 copy-done
  263.2 1.7 copy.24
  (1 shorter events, 0.0 us)
Async XLA Ops:
  258.3 4.8 %copy-start = (bf16[1536,1024]{1,0:T(8,128)(2,1)S(1)}, bf16[1536,1024]{1,0:T(8,128)(2,1)}, u32[]{:S(2)}) copy-start(bf16[1536,1024]{1,0:T(8,128)(2,1)} %get-tuple-element.16) | copy-start | bytes 9437188

commit v2 on v1

--- a/solution.py
+++ b/solution.py
@@ -22,9 +22,10 @@
 ROWS = 3072
 CHUNKS = ROWS // (2 * CROWS)
 SLOTS = 16
-STAGES = 8
 LAG = 2
 DP = 4
+OUT_SPACE = pltpu.VMEM
+VMEM_LIMIT = 54 * 2 ** 20
 STEPS = CHUNKS + 2 * LAG * (DP - 1)
 
 
@@ -40,11 +41,11 @@
     return lax.dot_general(a, b, (((0,), (0,)), ((), ())), preferred_element_type=F32)
 
 
-def layer_kernel(x_ref, h_ref, dy_ref, st_ref, gn_ref, wq_ref, wo_ref, w1_ref, w2_ref,
-                 dx_ref, fb_ref,
-                 gb, land, stage, nrm, part, recv_a, recv_b, recv_c, dh_f, dh_b,
-                 ch_send, ch_recv, ch_free, fb_send, fb_recv, st_copy,
-                 pa_send, pa_recv, pb_send, pb_recv, pd_send, pd_recv, dx_copy):
+def layer_kernel(x_hbm, h_hbm, dy_hbm, m1_ref, r1_ref, m2_ref, r2_ref, g1_ref, g2_ref, wq_hbm, wo_hbm, w1_hbm, w2_hbm,
+                 part, fb_ref,
+                 gb, land, nrm, recv_a, recv_b, recv_c, dh_f, dh_b, h_ref, dy_ref, st_ref, gn_ref,
+                 ch_send, ch_recv, ch_free, fb_send, fb_recv,
+                 pa_send, pa_recv, pb_send, pb_recv, pd_send, pd_recv, in_sem, mate_done):
     pod, z, tp = lax.axis_index('pod'), lax.axis_index('dp'), lax.axis_index('tp')
     core = lax.rem(tp, 2)
     mate = (pod, z, tp + 1 - 2 * core)
@@ -54,6 +55,19 @@
     own0 = core * HALF
     par0 = HALF - own0
 
+    def rows(i):
+        return pl.ds(pl.multiple_of(i * BLK, BLK), BLK)
+
+    def at(base, b):
+        return pl.ds(pl.multiple_of(base + b * BLK, BLK), BLK)
+
+    def h_copy(i):
+        return pltpu.make_async_copy(h_hbm.at[rows(i)], h_ref.at[rows(i)], in_sem.at[i])
+
+    dy_copy = pltpu.make_async_copy(dy_hbm, dy_ref, in_sem.at[6])
+    for i in range(NBLK):
+        h_copy(i).start()
+
     barrier = pltpu.get_barrier_semaphore()
     for dev in (mate, peer):
         pl.semaphore_signal(barrier, inc=1, device_id=dev, device_id_type=MESH)
@@ -75,19 +89,10 @@
             src_ref=gb.at[rows_of(way, c)], dst_ref=land.at[way, slot], send_sem=ch_send.at[way, slot],
             recv_sem=ch_recv.at[way, slot], device_id=nxt, device_id_type=MESH)
 
-    def total_copy(way, c, prv):
-        return pltpu.make_async_remote_copy(
-            src_ref=stage.at[way, lax.rem(c, STAGES)], dst_ref=fb_ref.at[rows_of(way, c)], send_sem=fb_send.at[way, c],
-            recv_sem=fb_recv.at[way, c], device_id=prv, device_id_type=MESH)
-
     def pass_copy(way, c, prv):
         return pltpu.make_async_remote_copy(
             src_ref=fb_ref.at[rows_of(way, c)], dst_ref=fb_ref.at[rows_of(way, c)], send_sem=fb_send.at[way, c],
             recv_sem=fb_recv.at[way, c], device_id=prv, device_id_type=MESH)
-
-    def keep_copy(way, c):
-        slot = lax.rem(c, STAGES)
-        return pltpu.make_async_copy(stage.at[way, slot], fb_ref.at[rows_of(way, c)], st_copy.at[way, slot])
 
     def chain_step(s):
         for way in (0, 1):
@@ -115,13 +120,8 @@
 
                 @pl.when(pos == DP - 1)
                 def _():
-                    @pl.when(c >= STAGES)
-                    def _():
-                        total_copy(way, c - STAGES, prv).wait_send()
-                        keep_copy(way, c - STAGES).wait()
-                    stage[way, lax.rem(c, STAGES)] = gb[rows_of(way, c), :].astype(BF16)
-                    total_copy(way, c, prv).start()
-                    keep_copy(way, c).start()
+                    fb_ref[rows_of(way, c), :] = gb[rows_of(way, c), :].astype(BF16)
+                    pass_copy(way, c, prv).start()
 
             c2 = s - LAG * (2 * (DP - 1) - pos)
 
@@ -150,27 +150,13 @@
                     return carry
                 lax.fori_loop(CHUNKS - SLOTS, CHUNKS, body, 0)
 
-            @pl.when(pos == DP - 1)
-            def _():
-                def body(c, carry):
-                    total_copy(way, c, prv).wait_send()
-                    keep_copy(way, c).wait()
-                    return carry
-                lax.fori_loop(CHUNKS - STAGES, CHUNKS, body, 0)
-
-            @pl.when((pos > 0) & (pos < DP - 1))
+            @pl.when(pos > 0)
             def _():
                 def body(c, carry):
                     pass_copy(way, c, prv).wait_send()
                     return carry
                 lax.fori_loop(0, CHUNKS, body, 0)
 
-    def rows(i):
-        return pl.ds(pl.multiple_of(i * BLK, BLK), BLK)
-
-    def at(base, b):
-        return pl.ds(pl.multiple_of(base + b * BLK, BLK), BLK)
-
     def hat(ref, rs, k):
         return (ref[rs, :].astype(F32) - st_ref[rs, k:k + 1]) * st_ref[rs, k + 1:k + 2]
 
@@ -181,7 +167,17 @@
         return rstd * (scaled - scaled_mean - x_hat * proj_mean)
 
     def gain(k):
-        return gn_ref[k:k + 1, :].astype(F32)
+        return gn_ref[k:k + 1, :]
+
+    def put_stats(k, ref):
+        stat_t = jnp.transpose(ref[...])
+        for b in range(TOK // 128):
+            st_ref[b * 128:(b + 1) * 128, k:k + 1] = stat_t[:, b:b + 1]
+
+    def put_gain(k, ref):
+        wide = ref[...].astype(F32)
+        for b in range(8):
+            gn_ref[k:k + 1, b * 128:(b + 1) * 128] = wide[b:b + 1, :]
 
     def mate_copy(rnd, b):
         return pltpu.make_async_remote_copy(
@@ -207,40 +203,68 @@
         ro = at(own0, b)
         part[ro, :] = fn(ro).astype(BF16)
 
-    def mlp(act_s, da_s):
-        def fwd(i, carry):
-            rs = rows(i)
-            n2 = (hat(h_ref, rs, 2) * gain(1)).astype(BF16)
-            nrm[rs, :] = n2
-            pre = dot_nn(n2, w1_ref[...]).astype(BF16).astype(F32)
-            th = jnp.tanh(GELU_C * (pre + 0.044715 * pre * pre * pre))
-            act_s[rs, :] = (0.5 * pre * (1.0 + th)).astype(BF16)
-            slope = 0.5 * (1.0 + th) + 0.5 * pre * (1.0 - th * th) * GELU_C * (1.0 + 0.134145 * pre * pre)
-            da_s[rs, :] = (dot_nt(dy_ref[rs, :], w2_ref[...]) * slope).astype(BF16)
-            return carry
-        lax.fori_loop(0, NBLK, fwd, 0)
-
-        def down(j, carry):
-            gb[rows(j), :] = dot_tn(act_s[:, rows(j)], dy_ref[...])
-            pl.when(lax.rem(j, 2) == 1)(lambda: chain_step(lax.div(j, 2)))
-            return carry
-        lax.fori_loop(0, DIM // BLK, down, 0)
+    def mlp(w1_ref, w2_ref, act_s, da_s):
+        def w1_copy(j):
+            return pltpu.make_async_copy(w1_hbm.at[:, rows(j)], w1_ref.at[:, rows(j)], in_sem.at[7 + j])
+
+        def w2_copy(j):
+            return pltpu.make_async_copy(w2_hbm.at[rows(j)], w2_ref.at[rows(j)], in_sem.at[11 + j])
+
+        w1_copy(0).start()
+        w2_copy(0).start()
+        dy_copy.start()
+        for j in range(1, 4):
+            w1_copy(j).start()
+            w2_copy(j).start()
+        put_stats(2, m2_ref)
+        put_stats(3, r2_ref)
+        put_gain(1, g2_ref)
+
+        def norm_two(i, carry):
+            h_copy(i).wait()
+            nrm[rows(i), :] = (hat(h_ref, rows(i), 2) * gain(1)).astype(BF16)
+            return carry
+        lax.fori_loop(0, NBLK, norm_two, 0)
+
+        def column(j, carry):
+            w1_copy(j).wait()
+            w2_copy(j).wait()
+            pl.when(j == 0)(lambda: dy_copy.wait())
+
+            def fwd(i, carry):
+                rs = pl.ds(pl.multiple_of(i * 512, 512), 512)
+                pre = dot_nn(nrm[rs, :], w1_ref[:, rows(j)]).astype(BF16).astype(F32)
+                th = jnp.tanh(GELU_C * (pre + 0.044715 * pre * pre * pre))
+                act_s[rs, :] = (0.5 * pre * (1.0 + th)).astype(BF16)
+                slope = 0.5 * (1.0 + th) + 0.5 * pre * (1.0 - th * th) * GELU_C * (1.0 + 0.134145 * pre * pre)
+                da_s[rs, rows(j)] = (dot_nt(dy_ref[rs, :], w2_ref[rows(j), :]) * slope).astype(BF16)
+                pl.when((i == 1) & (j > 0))(lambda: chain_step(2 * j - 1))
+                return carry
+            lax.fori_loop(0, 3, fwd, 0)
+            gb[rows(j), :] = dot_tn(act_s[...], dy_ref[...])
+            chain_step(2 * j)
+            return carry
+        lax.fori_loop(0, DIM // BLK, column, 0)
 
         def dn2(b, carry):
             part_block(0, b, lambda rs: dot_nt(da_s[rs, :], w1_ref[...]))
             pl.when(b > 0)(lambda: chip_sum(0, b - 1))
-            chain_step(2 + b)
+            chain_step(7 + b)
             return carry
         lax.fori_loop(0, HBLK, dn2, 0)
         chip_sum(0, HBLK - 1)
 
         def up(j, carry):
             gb[at(DIM, j), :] = dot_tn(nrm[:, rows(j)], da_s[...])
-            pl.when(lax.rem(j, 2) == 1)(lambda: chain_step(5 + lax.div(j, 2)))
+            pl.when(lax.rem(j, 2) == 1)(lambda: chain_step(10 + lax.div(j, 2)))
             return carry
         lax.fori_loop(0, DIM // BLK, up, 0)
 
-    pl.run_scoped(mlp, pltpu.VMEM((TOK, DIM), BF16), pltpu.VMEM((TOK, DIM), BF16))
+    pl.run_scoped(mlp, pltpu.VMEM((DIM, DIM), BF16), pltpu.VMEM((DIM, DIM), BF16),
+                  pltpu.VMEM((TOK, BLK), BF16), pltpu.VMEM((TOK, DIM), BF16))
+    put_stats(0, m1_ref)
+    put_stats(1, r1_ref)
+    put_gain(0, g1_ref)
 
     def mid_copy(b):
         return pltpu.make_async_remote_copy(
@@ -249,25 +273,31 @@
 
     def out_copy(b):
         return pltpu.make_async_remote_copy(
-            src_ref=part.at[at(own0, b)], dst_ref=dx_ref.at[at(own0, b)], send_sem=pd_send.at[1, b],
+            src_ref=part.at[at(own0, b)], dst_ref=part.at[at(own0, b)], send_sem=pd_send.at[1, b],
             recv_sem=pd_recv.at[1, b], device_id=mate, device_id_type=MESH)
 
-    def out_keep(b):
-        return pltpu.make_async_copy(part.at[at(own0, b)], dx_ref.at[at(own0, b)], dx_copy.at[b])
-
-    def attention(qkv, d_qkv, o_s, do_s, acc_k, acc_v):
+    def attention(x_ref, wq_ref, wo_ref, qkv, d_qkv, o_s, do_s, acc_k, acc_v):
+        x_copy = pltpu.make_async_copy(x_hbm, x_ref, in_sem.at[15])
+        wq_copy = pltpu.make_async_copy(wq_hbm, wq_ref, in_sem.at[16])
+        wo_copy = pltpu.make_async_copy(wo_hbm, wo_ref, in_sem.at[17])
+        x_copy.start()
+        wq_copy.start()
+        wo_copy.start()
+        x_copy.wait()
+        wq_copy.wait()
+        wo_copy.wait()
+
         def proj(i, carry):
             rs = rows(i)
             n1 = (hat(x_ref, rs, 0) * gain(0)).astype(BF16)
             nrm[rs, :] = n1
             qkv[rs, :] = dot_nt(n1, wq_ref[...]).astype(BF16)
-            pl.when(lax.rem(i, 2) == 1)(lambda: chain_step(7 + lax.div(i, 2)))
+            pl.when(lax.rem(i, 2) == 1)(lambda: chain_step(12 + lax.div(i, 2)))
             return carry
         lax.fori_loop(0, NBLK, proj, 0)
 
         def mid(b, carry):
-            chain_step(10 + 2 * b)
-            chain_step(11 + 2 * b)
+            chain_step(15 + b)
             peer_copy(0, b).wait_recv()
             ro = at(own0, b)
             d_norm = part[ro, :].astype(F32) + recv_b[b].astype(F32)
@@ -323,18 +353,18 @@
                         acc_k[0:span, :] += dk_h
                 o_s[rs, cols(0)] = jnp.where(lane < 64, outs[0], outs[1]).astype(BF16)
                 d_qkv[rs, cols(0)] = jnp.where(lane < 64, dqs[0], dqs[1]).astype(BF16)
-                chain_step(16 + p * NBLK + n)
+                chain_step(18 + p * NBLK + n)
             d_qkv[:, cols(1)] = acc_k[...].astype(BF16)
             d_qkv[:, cols(2)] = acc_v[...].astype(BF16)
             return carry
         lax.fori_loop(0, 2, pair, 0)
 
         gb[2 * DIM:2 * DIM + BLK, :] = dot_tn(o_s[...], dh_b[...])
-        chain_step(28)
+        chain_step(30)
 
         def w_qkv(j, carry):
             gb[at(2 * DIM + BLK, j), :] = dot_tn(d_qkv[:, rows(j)], nrm[...])
-            chain_step(29 + j)
+            chain_step(31 + j)
             return carry
         lax.fori_loop(0, 3, w_qkv, 0)
 
@@ -346,35 +376,38 @@
         def dn1(b, carry):
             part_block(1, b, lambda rs: dot_nn(d_qkv[rs, :], wq_ref[...]))
             pl.when(b > 0)(lambda: chip_sum(1, b - 1))
-            chain_step(32 + b)
+            chain_step(34 + b)
             return carry
         lax.fori_loop(0, HBLK, dn1, 0)
         chip_sum(1, HBLK - 1)
 
-    pl.run_scoped(attention, pltpu.VMEM((TOK, 768), BF16), pltpu.VMEM((TOK, 768), BF16),
+        def final(b, carry):
+            chain_step(37 + 3 * b)
+            chain_step(38 + 3 * b)
+            chain_step(39 + 3 * b)
+            peer_copy(1, b).wait_recv()
+            peer_copy(1, b).wait_send()
+            ro = at(own0, b)
+            d_norm = part[ro, :].astype(F32) + recv_c[b].astype(F32)
+            dx = dh_f[rows(b), :] + norm_back(d_norm, hat(x_ref, ro, 0), st_ref[ro, 1:2], gain(0))
+            part[ro, :] = dx.astype(BF16)
+            out_copy(b).start()
+            return carry
+        for b in range(HBLK):
+            mate_copy(1, b).wait_send()
+        pl.semaphore_signal(mate_done, inc=1, device_id=mate, device_id_type=MESH)
+        pl.semaphore_wait(mate_done, 1)
+        lax.fori_loop(0, HBLK, final, 0)
+
+    pl.run_scoped(attention, pltpu.VMEM((TOK, DIM), BF16), pltpu.VMEM((768, DIM), BF16), pltpu.VMEM((BLK, DIM), BF16),
+                  pltpu.VMEM((TOK, 768), BF16), pltpu.VMEM((TOK, 768), BF16),
                   pltpu.VMEM((TOK, BLK), BF16), pltpu.VMEM((TOK, BLK), BF16),
                   pltpu.VMEM((TOK, 128), F32), pltpu.VMEM((TOK, 128), F32))
 
-    def final(b, carry):
-        chain_step(35 + 3 * b)
-        chain_step(36 + 3 * b)
-        chain_step(37 + 3 * b)
-        peer_copy(1, b).wait_recv()
-        peer_copy(1, b).wait_send()
-        ro = at(own0, b)
-        d_norm = part[ro, :].astype(F32) + recv_c[b].astype(F32)
-        dx = dh_f[rows(b), :] + norm_back(d_norm, hat(x_ref, ro, 0), st_ref[ro, 1:2], gain(0))
-        part[ro, :] = dx.astype(BF16)
-        out_copy(b).start()
-        out_keep(b).start()
-        return carry
-    lax.fori_loop(0, HBLK, final, 0)
-    chain_steps(35 + 3 * HBLK, STEPS - 35 - 3 * HBLK)
+    chain_steps(37 + 3 * HBLK, STEPS - 37 - 3 * HBLK)
     chain_end()
     for b in range(HBLK):
-        mate_copy(1, b).wait_send()
         out_copy(b).wait()
-        out_keep(b).wait()
 
 
 def solution(mesh):
@@ -390,33 +423,34 @@
     scratch = [
         pltpu.VMEM((ROWS, DIM), F32),
         pltpu.VMEM((2, SLOTS, CROWS, DIM), F32),
-        pltpu.VMEM((2, STAGES, CROWS, DIM), BF16),
-        pltpu.VMEM((TOK, DIM), BF16),
         pltpu.VMEM((TOK, DIM), BF16),
         pltpu.VMEM((HBLK, BLK, DIM), BF16),
         pltpu.VMEM((HBLK, BLK, DIM), BF16),
         pltpu.VMEM((HBLK, BLK, DIM), BF16),
         pltpu.VMEM((HALF, DIM), F32),
         pltpu.VMEM((TOK, DIM), BF16),
+        pltpu.VMEM((TOK, DIM), BF16),
+        pltpu.VMEM((TOK, DIM), BF16),
+        pltpu.VMEM((TOK, 4), F32),
+        pltpu.VMEM((2, DIM), F32),
         dma((2, SLOTS)), dma((2, SLOTS)), pltpu.SemaphoreType.REGULAR((2,)),
-        dma((2, CHUNKS)), dma((2, CHUNKS)), dma((2, STAGES)),
+        dma((2, CHUNKS)), dma((2, CHUNKS)),
         dma((2, HBLK)), dma((2, HBLK)), dma((2, HBLK)), dma((2, HBLK)),
-        dma((2, HBLK)), dma((2, HBLK)), dma((HBLK,)),
+        dma((2, HBLK)), dma((2, HBLK)), dma((18,)), pltpu.SemaphoreType.REGULAR,
     ]
     layer = pl.pallas_call(
         layer_kernel,
-        out_shape=(jax.ShapeDtypeStruct((TOK, DIM), BF16), jax.ShapeDtypeStruct((ROWS, DIM), BF16)),
-        in_specs=[vmem] * 9,
-        out_specs=(hbm, hbm),
+        out_shape=(OUT_SPACE((TOK, DIM), BF16), OUT_SPACE((ROWS, DIM), BF16)),
+        in_specs=[hbm] * 3 + [vmem] * 6 + [hbm] * 4,
+        out_specs=(vmem, vmem),
         scratch_shapes=scratch,
-        compiler_params=pltpu.CompilerParams(collective_id=0, has_side_effects=True, vmem_limit_bytes=67043328),
+        compiler_params=pltpu.CompilerParams(collective_id=0, has_side_effects=True, vmem_limit_bytes=VMEM_LIMIT),
         name='layer_backward')
 
     def local_step(x_saved, h_saved, mean_one, rstd_one, mean_two, rstd_two, gain_one, gain_two, grad_y, w_qkv, w_proj, w_up, w_down):
-        stats = jnp.stack([mean_one, rstd_one, mean_two, rstd_two], axis=1)
-        gains = jnp.stack([gain_one, gain_two], axis=0)
+        small = [a.reshape(-1, 128) for a in (mean_one, rstd_one, mean_two, rstd_two, gain_one, gain_two)]
         wq_t = jnp.transpose(w_qkv, (1, 2, 3, 0)).reshape(768, DIM)
-        grad_x, grads = layer(x_saved, h_saved, grad_y, stats, gains, wq_t, w_proj.reshape(BLK, DIM), w_up, w_down)
+        grad_x, grads = layer(x_saved, h_saved, grad_y, *small, wq_t, w_proj.reshape(BLK, DIM), w_up, w_down)
         grad_qkv = jnp.transpose(grads[2 * DIM + BLK:].reshape(3, 4, 64, DIM), (3, 0, 1, 2))
         return (grad_x, grad_qkv, grads[2 * DIM:2 * DIM + BLK].reshape(4, 64, DIM), grads[DIM:2 * DIM], grads[:DIM])
 

time: 265 us -> 244 us (0.921)
  local copies, waits for them, and re-layouts: 16.4 us -> 6.2 us
  Pallas kernels: 247 us -> 237 us
    pallas_call x1, Pallas kernels: 247 us -> 237 us  [local_step(): layer(x_saved, h_saved, grad_y, *small, wq_t, w_proj.reshape(BLK, DIM), w...]
    another operation x7 -> x0, local copies, waits for them, and re-layouts: 5.36 us -> none  [the longest x5 3.99 us: local_step(): stats = jnp.stack([mean_one, rstd_one, mean_two, rstd_two], axis=1)]
where the time goes in v2:
time: 244 us
  Pallas kernels  237 us (97%)
  local copies, waits for them, and re-layouts  6.2 us (3%)
    pallas_call x1, Pallas kernels, local_step(): layer(x_saved, h_saved, grad_y, *small, wq_t, w_proj.reshape(BLK, DIM), w...  237 us

profile of v2, /device:TPU:0, one launch (start us, length us, event | category | flops | bytes accessed | tf_op | source)
XLA Modules:
  0.0 244.0 jit_solution(3905226420937857069)
XLA Ops:
  0.6 237.2 %layer_backward.1 = (bf16[1536,1024]{1,0:T(8,128)(2,1)S(1)}, bf16[3072,1024]{1,0:T(8,128)(2,1)S(1)}) custom-call(bf16[1536,1024]{1,0:T(8,128)(2,1)} %x_hbm.1, bf16[1536,1024]{1,0:T(8,128)(2,1)} %h_hbm.1, bf16[1536,1024]{1,0:T(8,128)(2,1)} %dy_hbm.1, f32[12,128]{1,0:T(8,128)} %bitcast.18, f32[12,128]{1,0:T(8,128)} %bitcast.19, f32[12,128]{1,0:T(8,128)} %bitcast.20, ...), custom_call_target="tpu_custom_call" | custom-call | tf_op jit(solution)/shard_map/layer_backward/pallas_call | solution.py:453
  237.8 1.7 copy.19
  239.5 0.8 slice.13
  240.3 1.3 slice.12
  241.6 2.4 %fusion = (bf16[1024,1024]{1,0:T(8,128)(2,1)}, bf16[1024,1024]{1,0:T(8,128)(2,1)}) fusion(bf16[3072,1024]{1,0:T(8,128)(2,1)S(1)} %get-tuple-element.8), kind=kLoop, calls=%fused_computation | loop fusion | bytes 8388608 | tf_op jit(solution)/shard_map/slice | solution.py:455

commit v3 on v2

--- a/solution.py
+++ b/solution.py
@@ -19,14 +19,19 @@
 NBLK = TOK // BLK
 HBLK = HALF // BLK
 CROWS = 32
+SROWS = 16
+SMALL = 8
 ROWS = 3072
-CHUNKS = ROWS // (2 * CROWS)
-SLOTS = 16
+CHUNKS = SMALL + (ROWS - 2 * SROWS * SMALL) // (2 * CROWS)
+SLOTS = 8
 LAG = 2
+LAG_BACK = 3
+HOLD = 0
 DP = 4
 OUT_SPACE = pltpu.VMEM
 VMEM_LIMIT = 54 * 2 ** 20
-STEPS = CHUNKS + 2 * LAG * (DP - 1)
+CLOSE_LIMIT = 1 * 2 ** 20
+STEPS = CHUNKS + (LAG + LAG_BACK) * (DP - 1) + HOLD
 
 
 def dot_nn(a, b):
@@ -64,47 +69,61 @@
     def h_copy(i):
         return pltpu.make_async_copy(h_hbm.at[rows(i)], h_ref.at[rows(i)], in_sem.at[i])
 
-    dy_copy = pltpu.make_async_copy(dy_hbm, dy_ref, in_sem.at[6])
-    for i in range(NBLK):
-        h_copy(i).start()
+    def dy_copy(i):
+        return pltpu.make_async_copy(dy_hbm.at[rows(i)], dy_ref.at[rows(i)], in_sem.at[18 + i])
 
     barrier = pltpu.get_barrier_semaphore()
     for dev in (mate, peer):
         pl.semaphore_signal(barrier, inc=1, device_id=dev, device_id_type=MESH)
     pl.when(z < DP - 1)(lambda: pl.semaphore_signal(barrier, inc=1, device_id=(pod, z_hi, tp), device_id_type=MESH))
     pl.when(z > 0)(lambda: pl.semaphore_signal(barrier, inc=1, device_id=(pod, z_lo, tp), device_id_type=MESH))
-    pl.semaphore_wait(barrier, 2 + jnp.where(z < DP - 1, 1, 0) + jnp.where(z > 0, 1, 0))
+    peers = 2 + jnp.where(z < DP - 1, 1, 0) + jnp.where(z > 0, 1, 0)
 
     def way_of(way):
         if way == 0:
             return z, (pod, z_hi, tp), (pod, z_lo, tp)
         return DP - 1 - z, (pod, z_lo, tp), (pod, z_hi, tp)
 
-    def rows_of(way, c):
-        return pl.ds(pl.multiple_of(c * (2 * CROWS) + way * CROWS, CROWS), CROWS)
-
-    def chain_copy(way, c, nxt):
+    def rows_of(way, c, big):
+        if big:
+            start = 2 * SROWS * SMALL + (c - SMALL) * (2 * CROWS) + way * CROWS
+            return pl.ds(pl.multiple_of(start, CROWS), CROWS)
+        return pl.ds(pl.multiple_of(c * (2 * SROWS) + way * SROWS, SROWS), SROWS)
+
+    def land_at(way, c, big):
+        return land.at[way, lax.rem(c, SLOTS), pl.ds(0, CROWS if big else SROWS)]
+
+    def chain_copy(way, c, nxt, big):
         slot = lax.rem(c, SLOTS)
         return pltpu.make_async_remote_copy(
-            src_ref=gb.at[rows_of(way, c)], dst_ref=land.at[way, slot], send_sem=ch_send.at[way, slot],
+            src_ref=gb.at[rows_of(way, c, big)], dst_ref=land_at(way, c, big), send_sem=ch_send.at[way, slot],
             recv_sem=ch_recv.at[way, slot], device_id=nxt, device_id_type=MESH)
 
-    def pass_copy(way, c, prv):
+    def pass_copy(way, c, prv, big):
         return pltpu.make_async_remote_copy(
-            src_ref=fb_ref.at[rows_of(way, c)], dst_ref=fb_ref.at[rows_of(way, c)], send_sem=fb_send.at[way, c],
+            src_ref=fb_ref.at[rows_of(way, c, big)], dst_ref=fb_ref.at[rows_of(way, c, big)], send_sem=fb_send.at[way, c],
             recv_sem=fb_recv.at[way, c], device_id=prv, device_id_type=MESH)
 
-    def chain_step(s):
+    def chain_step(s, early=False):
         for way in (0, 1):
             pos, nxt, prv = way_of(way)
             c = s - LAG * pos
 
-            @pl.when((c >= 0) & (c < CHUNKS))
-            def _():
+            def reduce_step(big):
+                rs = rows_of(way, c, big)
+
                 @pl.when(pos > 0)
                 def _():
-                    chain_copy(way, c, nxt).wait_recv()
-                    gb[rows_of(way, c), :] += land[way, lax.rem(c, SLOTS)]
+                    chain_copy(way, c, nxt, big).wait_recv()
+                    total = gb[rs, :] + land_at(way, c, big)[...]
+
+                    @pl.when(pos < DP - 1)
+                    def _():
+                        gb[rs, :] = total
+
+                    @pl.when(pos == DP - 1)
+                    def _():
+                        fb_ref[rs, :] = total.astype(BF16)
 
                     @pl.when(c < CHUNKS - SLOTS)
                     def _():
@@ -115,23 +134,25 @@
                     @pl.when(c >= SLOTS)
                     def _():
                         pl.semaphore_wait(ch_free.at[way], 1)
-                        chain_copy(way, c - SLOTS, nxt).wait_send()
-                    chain_copy(way, c, nxt).start()
-
-                @pl.when(pos == DP - 1)
-                def _():
-                    fb_ref[rows_of(way, c), :] = gb[rows_of(way, c), :].astype(BF16)
-                    pass_copy(way, c, prv).start()
-
-            c2 = s - LAG * (2 * (DP - 1) - pos)
-
-            @pl.when((pos < DP - 1) & (c2 >= 0) & (c2 < CHUNKS))
-            def _():
-                pass_copy(way, c2, prv).wait_recv()
+                    pl.when((c >= SLOTS) & (c < SLOTS + SMALL))(lambda: chain_copy(way, c - SLOTS, nxt, False).wait_send())
+                    pl.when(c >= SLOTS + SMALL)(lambda: chain_copy(way, c - SLOTS, nxt, True).wait_send())
+                    chain_copy(way, c, nxt, big).start()
+
+            if early:
+                pl.when((c >= 0) & (c < SMALL))(lambda: reduce_step(False))
+            pl.when((c >= SMALL) & (c < CHUNKS))(lambda: reduce_step(True))
+
+            c2 = s - HOLD - LAG * (DP - 1) - LAG_BACK * (DP - 1 - pos)
+
+            def pass_step(big):
+                pl.when(pos < DP - 1)(lambda: pass_copy(way, c2, prv, big).wait_recv())
 
                 @pl.when(pos > 0)
                 def _():
-                    pass_copy(way, c2, prv).start()
+                    pass_copy(way, c2, prv, big).start()
+
+            pl.when((c2 >= 0) & (c2 < SMALL))(lambda: pass_step(False))
+            pl.when((c2 >= SMALL) & (c2 < CHUNKS))(lambda: pass_step(True))
 
     def chain_steps(s0, n):
         def body(k, carry):
@@ -146,16 +167,17 @@
             @pl.when(pos < DP - 1)
             def _():
                 def body(c, carry):
-                    chain_copy(way, c, nxt).wait_send()
+                    chain_copy(way, c, nxt, True).wait_send()
                     return carry
                 lax.fori_loop(CHUNKS - SLOTS, CHUNKS, body, 0)
 
             @pl.when(pos > 0)
             def _():
-                def body(c, carry):
-                    pass_copy(way, c, prv).wait_send()
+                def body(c, carry, big):
+                    pass_copy(way, c, prv, big).wait_send()
                     return carry
-                lax.fori_loop(0, CHUNKS, body, 0)
+                lax.fori_loop(0, SMALL, functools.partial(body, big=False), 0)
+                lax.fori_loop(SMALL, CHUNKS, functools.partial(body, big=True), 0)
 
     def hat(ref, rs, k):
         return (ref[rs, :].astype(F32) - st_ref[rs, k:k + 1]) * st_ref[rs, k + 1:k + 2]
@@ -210,9 +232,12 @@
         def w2_copy(j):
             return pltpu.make_async_copy(w2_hbm.at[rows(j)], w2_ref.at[rows(j)], in_sem.at[11 + j])
 
-        w1_copy(0).start()
-        w2_copy(0).start()
-        dy_copy.start()
+        for i in range(NBLK):
+            h_copy(i).start()
+            if i == 0:
+                w1_copy(0).start()
+                w2_copy(0).start()
+            dy_copy(i).start()
         for j in range(1, 4):
             w1_copy(j).start()
             w2_copy(j).start()
@@ -220,43 +245,56 @@
         put_stats(3, r2_ref)
         put_gain(1, g2_ref)
 
-        def norm_two(i, carry):
+        def act_block(rs, n2, cols):
+            pre = dot_nn(n2, w1_ref[:, cols]).astype(BF16).astype(F32)
+            th = jnp.tanh(GELU_C * (pre + 0.044715 * pre * pre * pre))
+            act_s[rs, :] = (0.5 * pre * (1.0 + th)).astype(BF16)
+            slope = 0.5 * (1.0 + th) + 0.5 * pre * (1.0 - th * th) * GELU_C * (1.0 + 0.134145 * pre * pre)
+            da_s[rs, cols] = (dot_nt(dy_ref[rs, :], w2_ref[cols, :]) * slope).astype(BF16)
+
+        def first(i, carry):
             h_copy(i).wait()
-            nrm[rows(i), :] = (hat(h_ref, rows(i), 2) * gain(1)).astype(BF16)
-            return carry
-        lax.fori_loop(0, NBLK, norm_two, 0)
+            n2 = (hat(h_ref, rows(i), 2) * gain(1)).astype(BF16)
+            nrm[rows(i), :] = n2
+
+            @pl.when(i == 0)
+            def _():
+                w1_copy(0).wait()
+                w2_copy(0).wait()
+            dy_copy(i).wait()
+            act_block(rows(i), n2, slice(0, BLK))
+            return carry
+        lax.fori_loop(0, NBLK, first, 0)
+        gb[0:BLK, :] = dot_tn(act_s[...], dy_ref[...])
+        pl.semaphore_wait(barrier, peers)
+        chain_step(0, True)
 
         def column(j, carry):
             w1_copy(j).wait()
             w2_copy(j).wait()
-            pl.when(j == 0)(lambda: dy_copy.wait())
 
             def fwd(i, carry):
                 rs = pl.ds(pl.multiple_of(i * 512, 512), 512)
-                pre = dot_nn(nrm[rs, :], w1_ref[:, rows(j)]).astype(BF16).astype(F32)
-                th = jnp.tanh(GELU_C * (pre + 0.044715 * pre * pre * pre))
-                act_s[rs, :] = (0.5 * pre * (1.0 + th)).astype(BF16)
-                slope = 0.5 * (1.0 + th) + 0.5 * pre * (1.0 - th * th) * GELU_C * (1.0 + 0.134145 * pre * pre)
-                da_s[rs, rows(j)] = (dot_nt(dy_ref[rs, :], w2_ref[rows(j), :]) * slope).astype(BF16)
-                pl.when((i == 1) & (j > 0))(lambda: chain_step(2 * j - 1))
+                act_block(rs, nrm[rs, :], rows(j))
+                pl.when(i < 2)(lambda: chain_step(3 * j - 2 + i, True))
                 return carry
             lax.fori_loop(0, 3, fwd, 0)
             gb[rows(j), :] = dot_tn(act_s[...], dy_ref[...])
-            chain_step(2 * j)
-            return carry
-        lax.fori_loop(0, DIM // BLK, column, 0)
+            chain_step(3 * j, True)
+            return carry
+        lax.fori_loop(1, DIM // BLK, column, 0)
 
         def dn2(b, carry):
             part_block(0, b, lambda rs: dot_nt(da_s[rs, :], w1_ref[...]))
             pl.when(b > 0)(lambda: chip_sum(0, b - 1))
-            chain_step(7 + b)
+            chain_step(10 + b, True)
             return carry
         lax.fori_loop(0, HBLK, dn2, 0)
         chip_sum(0, HBLK - 1)
 
         def up(j, carry):
             gb[at(DIM, j), :] = dot_tn(nrm[:, rows(j)], da_s[...])
-            pl.when(lax.rem(j, 2) == 1)(lambda: chain_step(10 + lax.div(j, 2)))
+            pl.when(lax.rem(j, 2) == 1)(lambda: chain_step(13 + lax.div(j, 2), True))
             return carry
         lax.fori_loop(0, DIM // BLK, up, 0)
 
@@ -292,12 +330,13 @@
             n1 = (hat(x_ref, rs, 0) * gain(0)).astype(BF16)
             nrm[rs, :] = n1
             qkv[rs, :] = dot_nt(n1, wq_ref[...]).astype(BF16)
-            pl.when(lax.rem(i, 2) == 1)(lambda: chain_step(12 + lax.div(i, 2)))
+            pl.when((i == 2) | (i == 4))(lambda: chain_step(14 + lax.div(i, 2), True))
             return carry
         lax.fori_loop(0, NBLK, proj, 0)
 
         def mid(b, carry):
-            chain_step(15 + b)
+            chain_step(17 + 2 * b)
+            pl.when(b < 2)(lambda: chain_step(18 + 2 * b))
             peer_copy(0, b).wait_recv()
             ro = at(own0, b)
             d_norm = part[ro, :].astype(F32) + recv_b[b].astype(F32)
@@ -322,7 +361,8 @@
         def pair(p, carry):
             def cols(k):
                 return pl.ds(pl.multiple_of(k * 256 + p * 128, 128), 128)
-            for n, i in enumerate(reversed(range(NBLK))):
+            polls = 0
+            for i in reversed(range(NBLK)):
                 span = (i + 1) * BLK
                 rs = slice(i * BLK, span)
                 k_all = qkv[0:span, cols(1)]
@@ -351,20 +391,22 @@
                     else:
                         acc_v[0:span, :] += dv_h
                         acc_k[0:span, :] += dk_h
+                    if (i >= 4 and hh == 0) or (i >= 2 and hh == 1) or (i == 0 and hh == 1):
+                        chain_step(22 + p * 7 + polls)
+                        polls += 1
                 o_s[rs, cols(0)] = jnp.where(lane < 64, outs[0], outs[1]).astype(BF16)
                 d_qkv[rs, cols(0)] = jnp.where(lane < 64, dqs[0], dqs[1]).astype(BF16)
-                chain_step(18 + p * NBLK + n)
             d_qkv[:, cols(1)] = acc_k[...].astype(BF16)
             d_qkv[:, cols(2)] = acc_v[...].astype(BF16)
             return carry
         lax.fori_loop(0, 2, pair, 0)
 
         gb[2 * DIM:2 * DIM + BLK, :] = dot_tn(o_s[...], dh_b[...])
-        chain_step(30)
+        chain_step(36)
 
         def w_qkv(j, carry):
             gb[at(2 * DIM + BLK, j), :] = dot_tn(d_qkv[:, rows(j)], nrm[...])
-            chain_step(31 + j)
+            chain_step(37 + j)
             return carry
         lax.fori_loop(0, 3, w_qkv, 0)
 
@@ -376,15 +418,15 @@
         def dn1(b, carry):
             part_block(1, b, lambda rs: dot_nn(d_qkv[rs, :], wq_ref[...]))
             pl.when(b > 0)(lambda: chip_sum(1, b - 1))
-            chain_step(34 + b)
+            chain_step(40 + b)
             return carry
         lax.fori_loop(0, HBLK, dn1, 0)
         chip_sum(1, HBLK - 1)
 
         def final(b, carry):
-            chain_step(37 + 3 * b)
-            chain_step(38 + 3 * b)
-            chain_step(39 + 3 * b)
+            chain_step(43 + 3 * b)
+            chain_step(44 + 3 * b)
+            chain_step(45 + 3 * b)
             peer_copy(1, b).wait_recv()
             peer_copy(1, b).wait_send()
             ro = at(own0, b)
@@ -404,10 +446,22 @@
                   pltpu.VMEM((TOK, BLK), BF16), pltpu.VMEM((TOK, BLK), BF16),
                   pltpu.VMEM((TOK, 128), F32), pltpu.VMEM((TOK, 128), F32))
 
-    chain_steps(37 + 3 * HBLK, STEPS - 37 - 3 * HBLK)
+    chain_steps(43 + 3 * HBLK, STEPS - 43 - 3 * HBLK)
     chain_end()
     for b in range(HBLK):
         out_copy(b).wait()
+
+
+def close_kernel(dx_ref, fb_ref, x_out, q_out, o_out, up_out, down_out, sem):
+    copies = [pltpu.make_async_copy(fb_ref.at[0:DIM], down_out, sem.at[0]),
+              pltpu.make_async_copy(fb_ref.at[DIM:2 * DIM], up_out, sem.at[1]),
+              pltpu.make_async_copy(dx_ref, x_out, sem.at[2]),
+              pltpu.make_async_copy(fb_ref.at[2 * DIM:2 * DIM + BLK], o_out, sem.at[3]),
+              pltpu.make_async_copy(fb_ref.at[2 * DIM + BLK:ROWS], q_out, sem.at[4])]
+    for copy in copies:
+        copy.start()
+    for copy in copies:
+        copy.wait()
 
 
 def solution(mesh):
@@ -436,7 +490,7 @@
         dma((2, SLOTS)), dma((2, SLOTS)), pltpu.SemaphoreType.REGULAR((2,)),
         dma((2, CHUNKS)), dma((2, CHUNKS)),
         dma((2, HBLK)), dma((2, HBLK)), dma((2, HBLK)), dma((2, HBLK)),
-        dma((2, HBLK)), dma((2, HBLK)), dma((18,)), pltpu.SemaphoreType.REGULAR,
+        dma((2, HBLK)), dma((2, HBLK)), dma((24,)), pltpu.SemaphoreType.REGULAR,
     ]
     layer = pl.pallas_call(
         layer_kernel,
@@ -447,11 +501,21 @@
         compiler_params=pltpu.CompilerParams(collective_id=0, has_side_effects=True, vmem_limit_bytes=VMEM_LIMIT),
         name='layer_backward')
 
+    close = pl.pallas_call(
+        close_kernel,
+        out_shape=tuple(jax.ShapeDtypeStruct((r, DIM), BF16) for r in (TOK, 768, BLK, DIM, DIM)),
+        in_specs=[vmem, vmem],
+        out_specs=(hbm,) * 5,
+        scratch_shapes=[dma((5,))],
+        compiler_params=pltpu.CompilerParams(vmem_limit_bytes=CLOSE_LIMIT),
+        name='close')
+
     def local_step(x_saved, h_saved, mean_one, rstd_one, mean_two, rstd_two, gain_one, gain_two, grad_y, w_qkv, w_proj, w_up, w_down):
         small = [a.reshape(-1, 128) for a in (mean_one, rstd_one, mean_two, rstd_two, gain_one, gain_two)]
         wq_t = jnp.transpose(w_qkv, (1, 2, 3, 0)).reshape(768, DIM)
         grad_x, grads = layer(x_saved, h_saved, grad_y, *small, wq_t, w_proj.reshape(BLK, DIM), w_up, w_down)
-        grad_qkv = jnp.transpose(grads[2 * DIM + BLK:].reshape(3, 4, 64, DIM), (3, 0, 1, 2))
-        return (grad_x, grad_qkv, grads[2 * DIM:2 * DIM + BLK].reshape(4, 64, DIM), grads[DIM:2 * DIM], grads[:DIM])
+        grad_x, grad_qkv, grad_proj, grad_up, grad_down = close(grad_x, grads)
+        grad_qkv = jnp.transpose(grad_qkv.reshape(3, 4, 64, DIM), (3, 0, 1, 2))
+        return grad_x, grad_qkv, grad_proj.reshape(4, 64, DIM), grad_up, grad_down
 
     return jax.shard_map(local_step, mesh=mesh, in_specs=in_specs, out_specs=out_specs, check_vma=False)

time: 244 us -> 242 us (level)
  local copies, waits for them, and re-layouts: 6.2 us -> 0 us
  Pallas kernels: 237 us -> 241 us
    slice x3 -> x0, local copies, waits for them, and re-layouts: 4.54 us -> none  [the longest x1 2.45 us: local_step(): grads[:DIM]]
    pallas_call x0 -> x1, Pallas kernels: none -> 3.67 us  [local_step(): grad_x, grad_qkv, grad_proj, grad_up, grad_down = close(grad_x, grads)]
where the time goes in v3:
time: 242 us
  Pallas kernels  241 us (100%)
    pallas_call x1, Pallas kernels, local_step(): layer(x_saved, h_saved, grad_y, *small, wq_t, w_proj.reshape(BLK, DIM), w...  237 us

profile of v3, /device:TPU:0, one launch (start us, length us, event | category | flops | bytes accessed | tf_op | source)
XLA Modules:
  0.0 241.6 jit_solution(18438192649648513370)
XLA Ops:
  0.6 237.1 %layer_backward.1 = (bf16[1536,1024]{1,0:T(8,128)(2,1)S(1)}, bf16[3072,1024]{1,0:T(8,128)(2,1)S(1)}) custom-call(bf16[1536,1024]{1,0:T(8,128)(2,1)} %x_hbm.1, bf16[1536,1024]{1,0:T(8,128)(2,1)} %h_hbm.1, bf16[1536,1024]{1,0:T(8,128)(2,1)} %dy_hbm.1, f32[12,128]{1,0:T(8,128)} %bitcast.16, f32[12,128]{1,0:T(8,128)} %bitcast.17, f32[12,128]{1,0:T(8,128)} %bitcast.18, ...), custom_call_target="tpu_custom_call" | custom-call | tf_op jit(solution)/shard_map/layer_backward/pallas_call | solution.py:516
  237.8 3.7 %close.1 = (bf16[1536,1024]{1,0:T(8,128)(2,1)}, bf16[768,1024]{1,0:T(8,128)(2,1)}, bf16[256,1024]{1,0:T(8,128)(2,1)}, bf16[1024,1024]{1,0:T(8,128)(2,1)}, bf16[1024,1024]{1,0:T(8,128)(2,1)}) custom-call(bf16[1536,1024]{1,0:T(8,128)(2,1)S(1)} %get-tuple-element.12.dx_ref, bf16[3072,1024]{1,0:T(8,128)(2,1)S(1)} %get-tuple-element.13.fb_ref), custom_call_target="tpu_custom_call" | custom-call | tf_op jit(solution)/shard_map/close/pallas_call | solution.py:517

commit v4 on v3

--- a/solution.py
+++ b/solution.py
@@ -25,7 +25,7 @@
 CHUNKS = SMALL + (ROWS - 2 * SROWS * SMALL) // (2 * CROWS)
 SLOTS = 8
 LAG = 2
-LAG_BACK = 3
+LAG_BACK = 2
 HOLD = 0
 DP = 4
 OUT_SPACE = pltpu.VMEM

time: 242 us -> 241 us (level)
  no operation moved by 1% of the time
where the time goes in v4:
time: 241 us
  Pallas kernels  240 us (100%)
    pallas_call x1, Pallas kernels, local_step(): layer(x_saved, h_saved, grad_y, *small, wq_t, w_proj.reshape(BLK, DIM), w...  236 us

profile of v4, /device:TPU:0, one launch (start us, length us, event | category | flops | bytes accessed | tf_op | source)
XLA Modules:
  0.0 240.5 jit_solution(12405404552760428412)
XLA Ops:
  0.6 236.0 %layer_backward.1 = (bf16[1536,1024]{1,0:T(8,128)(2,1)S(1)}, bf16[3072,1024]{1,0:T(8,128)(2,1)S(1)}) custom-call(bf16[1536,1024]{1,0:T(8,128)(2,1)} %x_hbm.1, bf16[1536,1024]{1,0:T(8,128)(2,1)} %h_hbm.1, bf16[1536,1024]{1,0:T(8,128)(2,1)} %dy_hbm.1, f32[12,128]{1,0:T(8,128)} %bitcast.16, f32[12,128]{1,0:T(8,128)} %bitcast.17, f32[12,128]{1,0:T(8,128)} %bitcast.18, ...), custom_call_target="tpu_custom_call" | custom-call | tf_op jit(solution)/shard_map/layer_backward/pallas_call | solution.py:516
  236.7 3.7 %close.1 = (bf16[1536,1024]{1,0:T(8,128)(2,1)}, bf16[768,1024]{1,0:T(8,128)(2,1)}, bf16[256,1024]{1,0:T(8,128)(2,1)}, bf16[1024,1024]{1,0:T(8,128)(2,1)}, bf16[1024,1024]{1,0:T(8,128)(2,1)}) custom-call(bf16[1536,1024]{1,0:T(8,128)(2,1)S(1)} %get-tuple-element.12.dx_ref, bf16[3072,1024]{1,0:T(8,128)(2,1)S(1)} %get-tuple-element.13.fb_ref), custom_call_target="tpu_custom_call" | custom-call | tf_op jit(solution)/shard_map/close/pallas_call | solution.py:517
